TPU v7x, 32 devices: a whole 2x2x4 slice. The times are simulated.
32 devices in a mesh: orb: 4 (over x, core), gx: 2 (over y), gyz: 4 (over z).
Axes of the slice: x: 2, y: 2, z: 4, core: 2. Of those that a mesh axis runs over, the one named last changes fastest.
Arguments:
- orbitals: float32 [2, 12, 32, 32, 128], P(None, 'orb', 'gx', 'gyz'), parts along dimension 1, may hold values from -12 to 12
- potential: float32 [32, 32, 128], P('gx', 'gyz'), may hold values from -8 to 60
Outputs:
- evolved: float32 [2, 12, 32, 32, 128], P(None, 'orb', 'gx', 'gyz'), parts along dimension 1
- residual: float32 [2, 12, 32, 32, 128], P(None, 'orb', 'gx', 'gyz'), parts along dimension 1
There are 4 independent parts, one for each index of `orb`. A program takes and returns all parts, laid end to end along the dimension named above; an argument that names none is the same for every part. Nothing has to cross between parts.
All inputs are finite; a program needn't handle non-finite values.
Results may differ from a plain program's by a relative error of at most 0.0003.
Values sent between devices are 32-bit elements; how exact they have to be, the bound alone decides.
A program may use at most 64 MiB of HBM per device.

v0:
```python
import jax
import jax.numpy as jnp
from jax import lax
from jax.sharding import PartitionSpec as P

ITERS = 4
SPACING = 0.25
HALF_STEP = 0.05
COEFF_NEAR = 4.0 / 3.0
COEFF_FAR = -1.0 / 12.0
COEFF_SELF = -2.5


def with_halo(array, sides, width):
    for axis, dim in sides:
        size, length = (lax.axis_size(axis), array.shape[dim])
        up = [(i, (i + 1) % size) for i in range(size - 1)]
        down = [(j, i) for i, j in up]
        last = lax.slice_in_dim(array, length - width, length, axis=dim)
        leading = lax.slice_in_dim(array, 0, width, axis=dim)
        before = lax.ppermute(last, axis, up)
        after = lax.ppermute(leading, axis, down)
        array = jnp.concatenate([before, array, after], axis=dim)
    return array


def laplace_apply(padded, potential):
    extent = (padded.shape[2] - 4, padded.shape[3] - 4, padded.shape[4] - 4)

    def window(shift_x, shift_y, shift_z):
        return padded[
            :,
            :,
            2 + shift_x : 2 + shift_x + extent[0],
            2 + shift_y : 2 + shift_y + extent[1],
            2 + shift_z : 2 + shift_z + extent[2],
        ]

    center = window(0, 0, 0)
    summed = 3.0 * COEFF_SELF * center
    for offset, weight in ((1, COEFF_NEAR), (2, COEFF_FAR)):
        summed = summed + weight * (
            window(offset, 0, 0)
            + window(-offset, 0, 0)
            + window(0, offset, 0)
            + window(0, -offset, 0)
            + window(0, 0, offset)
            + window(0, 0, -offset)
        )
    return -0.5 / SPACING**2 * summed + potential * center


def pad_depth(vector):
    return jnp.pad(vector, ((0, 0), (0, 0), (0, 0), (0, 0), (2, 2)))


def system(vector, applied):
    return jnp.stack([vector[0] - HALF_STEP * applied[1], vector[1] + HALF_STEP * applied[0]])


def precondition(vector, potential):
    diagonal = HALF_STEP * (3.75 / SPACING**2 + potential)
    divisor = 1.0 + diagonal * diagonal
    return jnp.stack(
        [(vector[0] + diagonal * vector[1]) / divisor, (vector[1] - diagonal * vector[0]) / divisor]
    )


def braket(left, right):
    real_part = jnp.sum(left[0] * right[0] + left[1] * right[1], axis=(1, 2, 3))
    imag_part = jnp.sum(left[0] * right[1] - left[1] * right[0], axis=(1, 2, 3))
    return (real_part, imag_part)


def times_complex(first, second):
    return (
        first[0] * second[0] - first[1] * second[1],
        first[0] * second[1] + first[1] * second[0],
    )


def divide_complex(first, second):
    modulus = second[0] * second[0] + second[1] * second[1]
    return (
        (first[0] * second[0] + first[1] * second[1]) / modulus,
        (first[1] * second[0] - first[0] * second[1]) / modulus,
    )


def scale_complex(coeff, vector):
    real_coef = coeff[0][:, None, None, None]
    imag_coef = coeff[1][:, None, None, None]
    return jnp.stack(
        [
            real_coef * vector[0] - imag_coef * vector[1],
            real_coef * vector[1] + imag_coef * vector[0],
        ]
    )


def shards(orbitals, potential):

    def apply_shallow(vector):
        padded = with_halo(vector, (("gx", 2), ("gyz", 3)), 2)
        return laplace_apply(pad_depth(padded), potential)

    h_orbitals = apply_shallow(orbitals)
    residual = jnp.stack([2.0 * HALF_STEP * h_orbitals[1], -2.0 * HALF_STEP * h_orbitals[0]])
    evolved = orbitals
    shadow = residual
    direction = residual
    rho_now = lax.psum(braket(shadow, residual), ("gx", "gyz"))
    for iteration in range(ITERS):
        dir_hat = precondition(direction, potential)
        image = system(dir_hat, apply_shallow(dir_hat))
        alpha_step = divide_complex(rho_now, lax.psum(braket(shadow, image), ("gx", "gyz")))
        half_step = residual - scale_complex(alpha_step, image)
        half_hat = precondition(half_step, potential)
        second = system(half_hat, apply_shallow(half_hat))
        cross_local = braket(second, half_step)
        norm_local = jnp.sum(second * second, axis=(0, 2, 3, 4))
        shadow_half = braket(shadow, half_step)
        shadow_second = braket(shadow, second)
        summed = lax.psum(
            (
                cross_local[0],
                cross_local[1],
                norm_local,
                shadow_half[0],
                shadow_half[1],
                shadow_second[0],
                shadow_second[1],
            ),
            ("gx", "gyz"),
        )
        cross_real, cross_imag, norm_second = (summed[0], summed[1], summed[2])
        omega_step = (cross_real / norm_second, cross_imag / norm_second)
        evolved = evolved + scale_complex(alpha_step, dir_hat) + scale_complex(omega_step, half_hat)
        residual = half_step - scale_complex(omega_step, second)
        if iteration + 1 < ITERS:
            along_second = times_complex(omega_step, (summed[5], summed[6]))
            rho_next = (summed[3] - along_second[0], summed[4] - along_second[1])
            beta_step = times_complex(
                divide_complex(rho_next, rho_now), divide_complex(alpha_step, omega_step)
            )
            direction = residual + scale_complex(
                beta_step, direction - scale_complex(omega_step, image)
            )
            rho_now = rho_next
    return (evolved, residual)


def solution(mesh):
    return jax.shard_map(
        shards,
        mesh=mesh,
        in_specs=(P(None, "orb", "gx", "gyz", None), P("gx", "gyz", None)),
        out_specs=(P(None, "orb", "gx", "gyz", None), P(None, "orb", "gx", "gyz", None)),
        check_vma=False,
    )
```

profile of v0, /device:TPU:0, one launch (start us, length us, event | category | flops | bytes accessed | tf_op | source)
XLA Modules:
  0.0 354.6 jit_solution(2603612143626635180)
XLA Ops:
  1.5 4.9 %collective-permute-start.1 = (f32[2,3,2,8,128]{4,3,2,1,0:T(8,128)S(1)}, f32[2,3,2,8,128]{4,3,2,1,0:T(8,128)S(1)}, u32[]{:S(2)}, u32[]{:S(2)}) collective-permute-start(f32[2,3,2,8,128]{4,3,2,1,0:T(8,128)S(1)} %get-tuple-element.244), channel_id=1, source_target_pairs={{0,4},{1,5},{2,6},{3,7},{8,12},{9,13},{10,14},{11,15},{16,20},{17,... | collective-permute-start | bytes 147464 | tf_op jit(solution)/shard_map/ppermute | solution.py:21
  18.4 4.4 %collective-permute-done.2 = f32[2,3,20,2,128]{4,3,2,1,0:T(2,128)S(1)} collective-permute-done((f32[2,3,20,2,128]{4,3,2,1,0:T(2,128)S(1)}, f32[2,3,20,2,128]{4,3,2,1,0:T(2,128)S(1)}, u32[]{:S(2)}, u32[]{:S(2)}) %collective-permute-start.2) | collective-permute-done | bytes 122912 | tf_op jit(solution)/shard_map/ppermute | solution.py:22
  27.9 4.3 %collective-permute-done.4 = f32[2,3,2,8,128]{4,3,2,1,0:T(8,128)S(1)} collective-permute-done((f32[2,3,2,8,128]{4,3,2,1,0:T(8,128)S(1)}, f32[2,3,2,8,128]{4,3,2,1,0:T(8,128)S(1)}, u32[]{:S(2)}, u32[]{:S(2)}) %collective-permute-start.4) | collective-permute-done | bytes 49184 | tf_op jit(solution)/shard_map/ppermute | solution.py:22
  38.2 4.4 %collective-permute-done.6 = f32[2,3,20,2,128]{4,3,2,1,0:T(2,128)S(1)} collective-permute-done((f32[2,3,20,2,128]{4,3,2,1,0:T(2,128)S(1)}, f32[2,3,20,2,128]{4,3,2,1,0:T(2,128)S(1)}, u32[]{:S(2)}, u32[]{:S(2)}) %collective-permute-start.6) | collective-permute-done | bytes 122912 | tf_op jit(solution)/shard_map/ppermute | solution.py:22
  44.6 18.8 %all-reduce.16 = (f32[3]{0:T(128)S(1)}, f32[3]{0:T(128)S(1)}, f32[3]{0:T(128)S(1)}, f32[3]{0:T(128)S(1)}) all-reduce(f32[3]{0:T(128)S(1)} %get-tuple-element.43, f32[3]{0:T(128)S(1)} %get-tuple-element.3, f32[3]{0:T(128)S(1)} %get-tuple-element.42, f32[3]{0:T(128)S(1)} %get-tuple-element.2), channel_id=1, replica_groups=mesh['orb'=4,'gx'=2,'gyz'=4] {'gx','gyz'}, use_global_device_ids=true, to_apply=%region_1.2 | all-reduce | flops 12 | bytes 96 | tf_op jit(solution)/shard_map/psum | solution.py:112
  68.0 4.3 %collective-permute-done.8 = f32[2,3,2,8,128]{4,3,2,1,0:T(8,128)S(1)} collective-permute-done((f32[2,3,2,8,128]{4,3,2,1,0:T(8,128)S(1)}, f32[2,3,2,8,128]{4,3,2,1,0:T(8,128)S(1)}, u32[]{:S(2)}, u32[]{:S(2)}) %collective-permute-start.8) | collective-permute-done | bytes 49184 | tf_op jit(solution)/shard_map/ppermute | solution.py:22
  76.9 4.4 %collective-permute-done.10 = f32[2,3,20,2,128]{4,3,2,1,0:T(2,128)S(1)} collective-permute-done((f32[2,3,20,2,128]{4,3,2,1,0:T(2,128)S(1)}, f32[2,3,20,2,128]{4,3,2,1,0:T(2,128)S(1)}, u32[]{:S(2)}, u32[]{:S(2)}) %collective-permute-start.10) | collective-permute-done | bytes 122912 | tf_op jit(solution)/shard_map/ppermute | solution.py:22
  83.6 17.2 %all-reduce.15 = (f32[3]{0:T(128)S(1)}, f32[3]{0:T(128)S(1)}, f32[3]{0:T(128)S(1)}, f32[3]{0:T(128)S(1)}, f32[3]{0:T(128)S(1)}, /*index=5*/f32[3]{0:T(128)S(1)}, f32[3]{0:T(128)S(1)}) all-reduce(f32[3]{0:T(128)S(1)} %get-tuple-element.40, f32[3]{0:T(128)S(1)} %fusion.80, ...), channel_id=1, replica_groups=mesh['orb'=4,'gx'=2,'gyz'=4] {'gx','gyz'}, use_global_device_ids=true, to_apply=%region_13.14 | all-reduce | flops 21 | bytes 168 | tf_op jit(solution)/shard_map/psum | solution.py:124
  108.5 4.3 %collective-permute-done.12 = f32[2,3,2,8,128]{4,3,2,1,0:T(8,128)S(1)} collective-permute-done((f32[2,3,2,8,128]{4,3,2,1,0:T(8,128)S(1)}, f32[2,3,2,8,128]{4,3,2,1,0:T(8,128)S(1)}, u32[]{:S(2)}, u32[]{:S(2)}) %collective-permute-start.12) | collective-permute-done | bytes 49184 | tf_op jit(solution)/shard_map/ppermute | solution.py:22
  116.9 4.4 %collective-permute-done.14 = f32[2,3,20,2,128]{4,3,2,1,0:T(2,128)S(1)} collective-permute-done((f32[2,3,20,2,128]{4,3,2,1,0:T(2,128)S(1)}, f32[2,3,20,2,128]{4,3,2,1,0:T(2,128)S(1)}, u32[]{:S(2)}, u32[]{:S(2)}) %collective-permute-start.14) | collective-permute-done | bytes 122912 | tf_op jit(solution)/shard_map/ppermute | solution.py:22
  123.3 17.2 %all-reduce.14 = (f32[3]{0:T(128)S(1)}, f32[3]{0:T(128)S(1)}) all-reduce(f32[3]{0:T(128)S(1)} %get-tuple-element.23, f32[3]{0:T(128)S(1)} %get-tuple-element.22), channel_id=1, replica_groups=mesh['orb'=4,'gx'=2,'gyz'=4] {'gx','gyz'}, use_global_device_ids=true, to_apply=%region_25.26 | all-reduce | flops 6 | bytes 48 | tf_op jit(solution)/shard_map/psum | solution.py:116
  147.8 4.3 %collective-permute-done.16 = f32[2,3,2,8,128]{4,3,2,1,0:T(8,128)S(1)} collective-permute-done((f32[2,3,2,8,128]{4,3,2,1,0:T(8,128)S(1)}, f32[2,3,2,8,128]{4,3,2,1,0:T(8,128)S(1)}, u32[]{:S(2)}, u32[]{:S(2)}) %collective-permute-start.16) | collective-permute-done | bytes 49184 | tf_op jit(solution)/shard_map/ppermute | solution.py:22
  156.3 4.4 %collective-permute-done.18 = f32[2,3,20,2,128]{4,3,2,1,0:T(2,128)S(1)} collective-permute-done((f32[2,3,20,2,128]{4,3,2,1,0:T(2,128)S(1)}, f32[2,3,20,2,128]{4,3,2,1,0:T(2,128)S(1)}, u32[]{:S(2)}, u32[]{:S(2)}) %collective-permute-start.18) | collective-permute-done | bytes 122912 | tf_op jit(solution)/shard_map/ppermute | solution.py:22
  163.6 17.4 %all-reduce.13 = (f32[3]{0:T(128)S(1)}, f32[3]{0:T(128)S(1)}, f32[3]{0:T(128)S(1)}, f32[3]{0:T(128)S(1)}, f32[3]{0:T(128)S(1)}, /*index=5*/f32[3]{0:T(128)S(1)}, f32[3]{0:T(128)S(1)}) all-reduce(f32[3]{0:T(128)} %get-tuple-element.36, f32[3]{0:T(128)S(1)} %fusion.81, ...), channel_id=1, replica_groups=mesh['orb'=4,'gx'=2,'gyz'=4] {'gx','gyz'}, use_global_device_ids=true, to_apply=%region_31.32 | all-reduce | flops 21 | bytes 168 | tf_op jit(solution)/shard_map/psum | solution.py:124
  199.5 4.4 %collective-permute-done.22 = f32[2,3,20,2,128]{4,3,2,1,0:T(2,128)S(1)} collective-permute-done((f32[2,3,20,2,128]{4,3,2,1,0:T(2,128)S(1)}, f32[2,3,20,2,128]{4,3,2,1,0:T(2,128)S(1)}, u32[]{:S(2)}, u32[]{:S(2)}) %collective-permute-start.22) | collective-permute-done | bytes 122912 | tf_op jit(solution)/shard_map/ppermute | solution.py:22
  205.9 17.3 %all-reduce.12 = (f32[3]{0:T(128)S(1)}, f32[3]{0:T(128)S(1)}) all-reduce(f32[3]{0:T(128)S(1)} %get-tuple-element.15, f32[3]{0:T(128)S(1)} %get-tuple-element.14), channel_id=1, replica_groups=mesh['orb'=4,'gx'=2,'gyz'=4] {'gx','gyz'}, use_global_device_ids=true, to_apply=%region_43.44 | all-reduce | flops 6 | bytes 48 | tf_op jit(solution)/shard_map/psum | solution.py:116
  230.6 4.3 %collective-permute-done.24 = f32[2,3,2,8,128]{4,3,2,1,0:T(8,128)S(1)} collective-permute-done((f32[2,3,2,8,128]{4,3,2,1,0:T(8,128)S(1)}, f32[2,3,2,8,128]{4,3,2,1,0:T(8,128)S(1)}, u32[]{:S(2)}, u32[]{:S(2)}) %collective-permute-start.24) | collective-permute-done | bytes 49184 | tf_op jit(solution)/shard_map/ppermute | solution.py:22
  239.0 4.6 %collective-permute-done.26 = f32[2,3,20,2,128]{4,3,2,1,0:T(2,128)S(1)} collective-permute-done((f32[2,3,20,2,128]{4,3,2,1,0:T(2,128)S(1)}, f32[2,3,20,2,128]{4,3,2,1,0:T(2,128)S(1)}, u32[]{:S(2)}, u32[]{:S(2)}) %collective-permute-start.26) | collective-permute-done | bytes 122912 | tf_op jit(solution)/shard_map/ppermute | solution.py:22
  247.1 18.0 %all-reduce.11 = (f32[3]{0:T(128)}, f32[3]{0:T(128)}, f32[3]{0:T(128)}, f32[3]{0:T(128)}, f32[3]{0:T(128)}, /*index=5*/f32[3]{0:T(128)}, f32[3]{0:T(128)}) all-reduce(f32[3]{0:T(128)} %get-tuple-element.32, f32[3]{0:T(128)} %fusion.82, f32[3]{0:T(128)} %get-tuple-element.33, ...), channel_id=1, replica_groups=mesh['orb'=4,'gx'=2,'gyz'=4] {'gx','gyz'}, use_global_device_ids=true, to_apply=%region_49.50 | all-reduce | flops 21 | bytes 168 | tf_op jit(solution)/shard_map/psum | solution.py:124
  283.5 4.4 %collective-permute-done.30 = f32[2,3,20,2,128]{4,3,2,1,0:T(2,128)S(1)} collective-permute-done((f32[2,3,20,2,128]{4,3,2,1,0:T(2,128)S(1)}, f32[2,3,20,2,128]{4,3,2,1,0:T(2,128)S(1)}, u32[]{:S(2)}, u32[]{:S(2)}) %collective-permute-start.30) | collective-permute-done | bytes 122912 | tf_op jit(solution)/shard_map/ppermute | solution.py:22
  290.4 17.4 %all-reduce.10 = (f32[3]{0:T(128)S(1)}, f32[3]{0:T(128)S(1)}) all-reduce(f32[3]{0:T(128)S(1)} %get-tuple-element.7, f32[3]{0:T(128)S(1)} %get-tuple-element.6), channel_id=1, replica_groups=mesh['orb'=4,'gx'=2,'gyz'=4] {'gx','gyz'}, use_global_device_ids=true, to_apply=%region_61.62 | all-reduce | flops 6 | bytes 48 | tf_op jit(solution)/shard_map/psum | solution.py:116
  317.2 4.3 %collective-permute-done.32 = f32[2,3,2,8,128]{4,3,2,1,0:T(8,128)S(1)} collective-permute-done((f32[2,3,2,8,128]{4,3,2,1,0:T(8,128)S(1)}, f32[2,3,2,8,128]{4,3,2,1,0:T(8,128)S(1)}, u32[]{:S(2)}, u32[]{:S(2)}) %collective-permute-start.32) | collective-permute-done | bytes 49184 | tf_op jit(solution)/shard_map/ppermute | solution.py:22
  325.7 4.4 %collective-permute-done.34 = f32[2,3,20,2,128]{4,3,2,1,0:T(2,128)S(1)} collective-permute-done((f32[2,3,20,2,128]{4,3,2,1,0:T(2,128)S(1)}, f32[2,3,20,2,128]{4,3,2,1,0:T(2,128)S(1)}, u32[]{:S(2)}, u32[]{:S(2)}) %collective-permute-start.34) | collective-permute-done | bytes 122912 | tf_op jit(solution)/shard_map/ppermute | solution.py:22
  332.9 17.2 %all-reduce.9 = (f32[3]{0:T(128)S(1)}, f32[3]{0:T(128)S(1)}, f32[3]{0:T(128)S(1)}) all-reduce(f32[3]{0:T(128)S(1)} %get-tuple-element.5, f32[3]{0:T(128)S(1)} %fusion.83, f32[3]{0:T(128)S(1)} %get-tuple-element.4), channel_id=1, replica_groups=mesh['orb'=4,'gx'=2,'gyz'=4] {'gx','gyz'}, use_global_device_ids=true, to_apply=%region_67.68 | all-reduce | flops 9 | bytes 72 | tf_op jit(solution)/shard_map/psum | solution.py:124
  (247 shorter events, 142.4 us)
Async XLA Ops:
  1.5 6.6 %collective-permute-start.1 = (f32[2,3,2,8,128]{4,3,2,1,0:T(8,128)S(1)}, f32[2,3,2,8,128]{4,3,2,1,0:T(8,128)S(1)}, u32[]{:S(2)}, u32[]{:S(2)}) collective-permute-start(f32[2,3,2,8,128]{4,3,2,1,0:T(8,128)S(1)} %get-tuple-element.244), channel_id=1, source_target_pairs={{0,4},{1,5},{2,6},{3,7},{8,12},{9,13},{10,14},{11,15},{16,20},{17,... | collective-permute-start | bytes 147464 | tf_op jit(solution)/shard_map/ppermute | solution.py:21
  6.4 6.0 %collective-permute-start = (f32[2,3,2,8,128]{4,3,2,1,0:T(8,128)S(1)}, f32[2,3,2,8,128]{4,3,2,1,0:T(8,128)S(1)}, u32[]{:S(2)}, u32[]{:S(2)}) collective-permute-start(f32[2,3,2,8,128]{4,3,2,1,0:T(8,128)S(1)} %get-tuple-element.243), channel_id=1, source_target_pairs={{4,0},{5,1},{6,2},{7,3},{12,8},{13,9},{14,10},{15,11},{20,16},{21,... | collective-permute-start | bytes 147464 | tf_op jit(solution)/shard_map/ppermute | solution.py:22
  12.5 5.9 %collective-permute-start.3 = (f32[2,3,20,2,128]{4,3,2,1,0:T(2,128)S(1)}, f32[2,3,20,2,128]{4,3,2,1,0:T(2,128)S(1)}, u32[]{:S(2)}, u32[]{:S(2)}) collective-permute-start(f32[2,3,20,2,128]{4,3,2,1,0:T(2,128)S(1)} %get-tuple-element.158), channel_id=1, source_target_pairs={{0,1},{1,2},{2,3},{4,5},{5,6},{6,7},{8,9},{9,10},{10,11},{12,13},{... | collective-permute-start | bytes 368648 | tf_op jit(solution)/shard_map/ppermute | solution.py:21
  16.0 6.8 %collective-permute-start.2 = (f32[2,3,20,2,128]{4,3,2,1,0:T(2,128)S(1)}, f32[2,3,20,2,128]{4,3,2,1,0:T(2,128)S(1)}, u32[]{:S(2)}, u32[]{:S(2)}) collective-permute-start(f32[2,3,20,2,128]{4,3,2,1,0:T(2,128)S(1)} %get-tuple-element.159), channel_id=1, source_target_pairs={{1,0},{2,1},{3,2},{5,4},{6,5},{7,6},{9,8},{10,9},{11,10},{13,12},{... | collective-permute-start | bytes 368648 | tf_op jit(solution)/shard_map/ppermute | solution.py:22
  26.2 6.0 %collective-permute-start.4 = (f32[2,3,2,8,128]{4,3,2,1,0:T(8,128)S(1)}, f32[2,3,2,8,128]{4,3,2,1,0:T(8,128)S(1)}, u32[]{:S(2)}, u32[]{:S(2)}) collective-permute-start(f32[2,3,2,8,128]{4,3,2,1,0:T(8,128)S(1)} %get-tuple-element.239), channel_id=1, source_target_pairs={{4,0},{5,1},{6,2},{7,3},{12,8},{13,9},{14,10},{15,11},{20,16},{21,... | collective-permute-start | bytes 147464 | tf_op jit(solution)/shard_map/ppermute | solution.py:22
  32.2 5.9 %collective-permute-start.7 = (f32[2,3,20,2,128]{4,3,2,1,0:T(2,128)S(1)}, f32[2,3,20,2,128]{4,3,2,1,0:T(2,128)S(1)}, u32[]{:S(2)}, u32[]{:S(2)}) collective-permute-start(f32[2,3,20,2,128]{4,3,2,1,0:T(2,128)S(1)} %get-tuple-element.156), channel_id=1, source_target_pairs={{0,1},{1,2},{2,3},{4,5},{5,6},{6,7},{8,9},{9,10},{10,11},{12,13},{... | collective-permute-start | bytes 368648 | tf_op jit(solution)/shard_map/ppermute | solution.py:21
  35.7 6.8 %collective-permute-start.6 = (f32[2,3,20,2,128]{4,3,2,1,0:T(2,128)S(1)}, f32[2,3,20,2,128]{4,3,2,1,0:T(2,128)S(1)}, u32[]{:S(2)}, u32[]{:S(2)}) collective-permute-start(f32[2,3,20,2,128]{4,3,2,1,0:T(2,128)S(1)} %get-tuple-element.157), channel_id=1, source_target_pairs={{1,0},{2,1},{3,2},{5,4},{6,5},{7,6},{9,8},{10,9},{11,10},{13,12},{... | collective-permute-start | bytes 368648 | tf_op jit(solution)/shard_map/ppermute | solution.py:22
  66.3 6.0 %collective-permute-start.8 = (f32[2,3,2,8,128]{4,3,2,1,0:T(8,128)S(1)}, f32[2,3,2,8,128]{4,3,2,1,0:T(8,128)S(1)}, u32[]{:S(2)}, u32[]{:S(2)}) collective-permute-start(f32[2,3,2,8,128]{4,3,2,1,0:T(8,128)S(1)} %get-tuple-element.233), channel_id=1, source_target_pairs={{4,0},{5,1},{6,2},{7,3},{12,8},{13,9},{14,10},{15,11},{20,16},{21,... | collective-permute-start | bytes 147464 | tf_op jit(solution)/shard_map/ppermute | solution.py:22
  74.5 6.8 %collective-permute-start.10 = (f32[2,3,20,2,128]{4,3,2,1,0:T(2,128)S(1)}, f32[2,3,20,2,128]{4,3,2,1,0:T(2,128)S(1)}, u32[]{:S(2)}, u32[]{:S(2)}) collective-permute-start(f32[2,3,20,2,128]{4,3,2,1,0:T(2,128)S(1)} %get-tuple-element.155), channel_id=1, source_target_pairs={{1,0},{2,1},{3,2},{5,4},{6,5},{7,6},{9,8},{10,9},{11,10},{13,12},{... | collective-permute-start | bytes 368648 | tf_op jit(solution)/shard_map/ppermute | solution.py:22
  106.7 6.0 %collective-permute-start.12 = (f32[2,3,2,8,128]{4,3,2,1,0:T(8,128)S(1)}, f32[2,3,2,8,128]{4,3,2,1,0:T(8,128)S(1)}, u32[]{:S(2)}, u32[]{:S(2)}) collective-permute-start(f32[2,3,2,8,128]{4,3,2,1,0:T(8,128)S(1)} %get-tuple-element.227), channel_id=1, source_target_pairs={{4,0},{5,1},{6,2},{7,3},{12,8},{13,9},{14,10},{15,11},{20,16},{21,... | collective-permute-start | bytes 147464 | tf_op jit(solution)/shard_map/ppermute | solution.py:22
  114.5 6.8 %collective-permute-start.14 = (f32[2,3,20,2,128]{4,3,2,1,0:T(2,128)S(1)}, f32[2,3,20,2,128]{4,3,2,1,0:T(2,128)S(1)}, u32[]{:S(2)}, u32[]{:S(2)}) collective-permute-start(f32[2,3,20,2,128]{4,3,2,1,0:T(2,128)S(1)} %get-tuple-element.153), channel_id=1, source_target_pairs={{1,0},{2,1},{3,2},{5,4},{6,5},{7,6},{9,8},{10,9},{11,10},{13,12},{... | collective-permute-start | bytes 368648 | tf_op jit(solution)/shard_map/ppermute | solution.py:22
  146.1 6.0 %collective-permute-start.16 = (f32[2,3,2,8,128]{4,3,2,1,0:T(8,128)S(1)}, f32[2,3,2,8,128]{4,3,2,1,0:T(8,128)S(1)}, u32[]{:S(2)}, u32[]{:S(2)}) collective-permute-start(f32[2,3,2,8,128]{4,3,2,1,0:T(8,128)S(1)} %get-tuple-element.223), channel_id=1, source_target_pairs={{4,0},{5,1},{6,2},{7,3},{12,8},{13,9},{14,10},{15,11},{20,16},{21,... | collective-permute-start | bytes 147464 | tf_op jit(solution)/shard_map/ppermute | solution.py:22
  153.9 6.8 %collective-permute-start.18 = (f32[2,3,20,2,128]{4,3,2,1,0:T(2,128)S(1)}, f32[2,3,20,2,128]{4,3,2,1,0:T(2,128)S(1)}, u32[]{:S(2)}, u32[]{:S(2)}) collective-permute-start(f32[2,3,20,2,128]{4,3,2,1,0:T(2,128)S(1)} %get-tuple-element.151), channel_id=1, source_target_pairs={{1,0},{2,1},{3,2},{5,4},{6,5},{7,6},{9,8},{10,9},{11,10},{13,12},{... | collective-permute-start | bytes 368648 | tf_op jit(solution)/shard_map/ppermute | solution.py:22
  185.6 5.7 %collective-permute-start.21 = (f32[2,3,2,8,128]{4,3,2,1,0:T(8,128)S(1)}, f32[2,3,2,8,128]{4,3,2,1,0:T(8,128)S(1)}, u32[]{:S(2)}, u32[]{:S(2)}) collective-permute-start(f32[2,3,2,8,128]{4,3,2,1,0:T(8,128)S(1)} %get-tuple-element.216), channel_id=1, source_target_pairs={{0,4},{1,5},{2,6},{3,7},{8,12},{9,13},{10,14},{11,15},{16,20},{17,... | collective-permute-start | bytes 147464 | tf_op jit(solution)/shard_map/ppermute | solution.py:21
  189.6 6.0 %collective-permute-start.20 = (f32[2,3,2,8,128]{4,3,2,1,0:T(8,128)S(1)}, f32[2,3,2,8,128]{4,3,2,1,0:T(8,128)S(1)}, u32[]{:S(2)}, u32[]{:S(2)}) collective-permute-start(f32[2,3,2,8,128]{4,3,2,1,0:T(8,128)S(1)} %get-tuple-element.217), channel_id=1, source_target_pairs={{4,0},{5,1},{6,2},{7,3},{12,8},{13,9},{14,10},{15,11},{20,16},{21,... | collective-permute-start | bytes 147464 | tf_op jit(solution)/shard_map/ppermute | solution.py:22
  197.1 6.8 %collective-permute-start.22 = (f32[2,3,20,2,128]{4,3,2,1,0:T(2,128)S(1)}, f32[2,3,20,2,128]{4,3,2,1,0:T(2,128)S(1)}, u32[]{:S(2)}, u32[]{:S(2)}) collective-permute-start(f32[2,3,20,2,128]{4,3,2,1,0:T(2,128)S(1)} %get-tuple-element.149), channel_id=1, source_target_pairs={{1,0},{2,1},{3,2},{5,4},{6,5},{7,6},{9,8},{10,9},{11,10},{13,12},{... | collective-permute-start | bytes 368648 | tf_op jit(solution)/shard_map/ppermute | solution.py:22
  225.0 5.6 %collective-permute-start.25 = (f32[2,3,2,8,128]{4,3,2,1,0:T(8,128)S(1)}, f32[2,3,2,8,128]{4,3,2,1,0:T(8,128)S(1)}, u32[]{:S(2)}, u32[]{:S(2)}) collective-permute-start(f32[2,3,2,8,128]{4,3,2,1,0:T(8,128)S(1)} %get-tuple-element.212), channel_id=1, source_target_pairs={{0,4},{1,5},{2,6},{3,7},{8,12},{9,13},{10,14},{11,15},{16,20},{17,... | collective-permute-start | bytes 147464 | tf_op jit(solution)/shard_map/ppermute | solution.py:21
  228.9 6.0 %collective-permute-start.24 = (f32[2,3,2,8,128]{4,3,2,1,0:T(8,128)S(1)}, f32[2,3,2,8,128]{4,3,2,1,0:T(8,128)S(1)}, u32[]{:S(2)}, u32[]{:S(2)}) collective-permute-start(f32[2,3,2,8,128]{4,3,2,1,0:T(8,128)S(1)} %get-tuple-element.213), channel_id=1, source_target_pairs={{4,0},{5,1},{6,2},{7,3},{12,8},{13,9},{14,10},{15,11},{20,16},{21,... | collective-permute-start | bytes 147464 | tf_op jit(solution)/shard_map/ppermute | solution.py:22
  236.6 7.0 %collective-permute-start.26 = (f32[2,3,20,2,128]{4,3,2,1,0:T(2,128)S(1)}, f32[2,3,20,2,128]{4,3,2,1,0:T(2,128)S(1)}, u32[]{:S(2)}, u32[]{:S(2)}) collective-permute-start(f32[2,3,20,2,128]{4,3,2,1,0:T(2,128)S(1)} %get-tuple-element.147), channel_id=1, source_target_pairs={{1,0},{2,1},{3,2},{5,4},{6,5},{7,6},{9,8},{10,9},{11,10},{13,12},{... | collective-permute-start | bytes 368648 | tf_op jit(solution)/shard_map/ppermute | solution.py:22
  273.3 6.0 %collective-permute-start.28 = (f32[2,3,2,8,128]{4,3,2,1,0:T(8,128)S(1)}, f32[2,3,2,8,128]{4,3,2,1,0:T(8,128)S(1)}, u32[]{:S(2)}, u32[]{:S(2)}) collective-permute-start(f32[2,3,2,8,128]{4,3,2,1,0:T(8,128)S(1)} %get-tuple-element.207), channel_id=1, source_target_pairs={{4,0},{5,1},{6,2},{7,3},{12,8},{13,9},{14,10},{15,11},{20,16},{21,... | collective-permute-start | bytes 147464 | tf_op jit(solution)/shard_map/ppermute | solution.py:22
  281.1 6.8 %collective-permute-start.30 = (f32[2,3,20,2,128]{4,3,2,1,0:T(2,128)S(1)}, f32[2,3,20,2,128]{4,3,2,1,0:T(2,128)S(1)}, u32[]{:S(2)}, u32[]{:S(2)}) collective-permute-start(f32[2,3,20,2,128]{4,3,2,1,0:T(2,128)S(1)} %get-tuple-element.145), channel_id=1, source_target_pairs={{1,0},{2,1},{3,2},{5,4},{6,5},{7,6},{9,8},{10,9},{11,10},{13,12},{... | collective-permute-start | bytes 368648 | tf_op jit(solution)/shard_map/ppermute | solution.py:22
  311.7 5.6 %collective-permute-start.33 = (f32[2,3,2,8,128]{4,3,2,1,0:T(8,128)S(1)}, f32[2,3,2,8,128]{4,3,2,1,0:T(8,128)S(1)}, u32[]{:S(2)}, u32[]{:S(2)}) collective-permute-start(f32[2,3,2,8,128]{4,3,2,1,0:T(8,128)S(1)} %get-tuple-element.202), channel_id=1, source_target_pairs={{0,4},{1,5},{2,6},{3,7},{8,12},{9,13},{10,14},{11,15},{16,20},{17,... | collective-permute-start | bytes 147464 | tf_op jit(solution)/shard_map/ppermute | solution.py:21
  315.5 6.0 %collective-permute-start.32 = (f32[2,3,2,8,128]{4,3,2,1,0:T(8,128)S(1)}, f32[2,3,2,8,128]{4,3,2,1,0:T(8,128)S(1)}, u32[]{:S(2)}, u32[]{:S(2)}) collective-permute-start(f32[2,3,2,8,128]{4,3,2,1,0:T(8,128)S(1)} %get-tuple-element.203), channel_id=1, source_target_pairs={{4,0},{5,1},{6,2},{7,3},{12,8},{13,9},{14,10},{15,11},{20,16},{21,... | collective-permute-start | bytes 147464 | tf_op jit(solution)/shard_map/ppermute | solution.py:22
  323.2 6.8 %collective-permute-start.34 = (f32[2,3,20,2,128]{4,3,2,1,0:T(2,128)S(1)}, f32[2,3,20,2,128]{4,3,2,1,0:T(2,128)S(1)}, u32[]{:S(2)}, u32[]{:S(2)}) collective-permute-start(f32[2,3,20,2,128]{4,3,2,1,0:T(2,128)S(1)} %get-tuple-element.143), channel_id=1, source_target_pairs={{1,0},{2,1},{3,2},{5,4},{6,5},{7,6},{9,8},{10,9},{11,10},{13,12},{... | collective-permute-start | bytes 368648 | tf_op jit(solution)/shard_map/ppermute | solution.py:22
  (50 other events, 290.0 us)
where the time goes:
time: 356 us; the launch traced here: 355 us
  blocking collectives  141 us (40%)
  waiting for transfers between devices  89.8 us (25%)
  starting transfers between devices  73.6 us (21%)
  other arithmetic  41.9 us (12%)
  local copies, waits for them, and re-layouts  6.87 us (2%)
    ppermute x18, waiting for transfers between devices, with_halo(): after = lax.ppermute(leading, axis, down)  76.6 us
    psum x4, blocking collectives, shards(): lax.psum((cross_local[0], cross_local[1], norm_local, shadow_half[0], sha...  69.8 us
    psum x3, blocking collectives, shards(): lax.psum(braket(shadow, image), ('gx', 'gyz'))  51.9 us
    ppermute x18, starting transfers between devices, with_halo(): before = lax.ppermute(last, axis, up)  50.2 us
    ppermute x18, starting transfers between devices, with_halo(): after = lax.ppermute(leading, axis, down)  23.4 us
    psum x1, blocking collectives, shards(): rho_now = lax.psum(braket(shadow, residual), ('gx', 'gyz'))  18.8 us
    ppermute x18, waiting for transfers between devices, with_halo(): before = lax.ppermute(last, axis, up)  13.2 us
    sub x11, other arithmetic, scale_complex(): real_coef * vector[0] - imag_coef * vector[1]  11.1 us
  transfers between devices with their start and end apart: 36, of which 36 were waited for; matrix products, arithmetic and copies ran while one was open for 0% of the time, Pallas kernels for 0%

commit v1 on v0

--- a/solution.py
+++ b/solution.py
@@ -9,6 +9,11 @@
 COEFF_NEAR = 4.0 / 3.0
 COEFF_FAR = -1.0 / 12.0
 COEFF_SELF = -2.5
+
+
+def axis_by_axis(value, one, other):
+    partial = lax.psum(value, one)
+    return lax.psum(partial, other)
 
 
 def with_halo(array, sides, width):
@@ -113,7 +118,7 @@
     for iteration in range(ITERS):
         dir_hat = precondition(direction, potential)
         image = system(dir_hat, apply_shallow(dir_hat))
-        alpha_step = divide_complex(rho_now, lax.psum(braket(shadow, image), ("gx", "gyz")))
+        alpha_step = divide_complex(rho_now, axis_by_axis(braket(shadow, image), "gyz", "gx"))
         half_step = residual - scale_complex(alpha_step, image)
         half_hat = precondition(half_step, potential)
         second = system(half_hat, apply_shallow(half_hat))

time: 356 us -> 360 us (1.011)
    psum x3 -> x8, blocking collectives: 51.9 us -> 56.6 us  [the longest x4 37 us: axis_by_axis(): partial = lax.psum(value, one)]
where the time goes in v1:
time: 360 us; the launch traced here: 359 us
  blocking collectives  144 us (40%)
  waiting for transfers between devices  90.5 us (25%)
  starting transfers between devices  73.6 us (20%)
  other arithmetic  42 us (12%)
  local copies, waits for them, and re-layouts  6.89 us (2%)
    ppermute x18, waiting for transfers between devices, with_halo(): after = lax.ppermute(leading, axis, down)  76.6 us
    psum x4, blocking collectives, shards(): lax.psum((cross_local[0], cross_local[1], norm_local, shadow_half[0], sha...  70 us
    ppermute x18, starting transfers between devices, with_halo(): before = lax.ppermute(last, axis, up)  49.9 us
    psum x4, blocking collectives, axis_by_axis(): partial = lax.psum(value, one)  37 us
    ppermute x18, starting transfers between devices, with_halo(): after = lax.ppermute(leading, axis, down)  23.7 us
    psum x4, blocking collectives, axis_by_axis(): return lax.psum(partial, other)  19.7 us
    psum x1, blocking collectives, shards(): rho_now = lax.psum(braket(shadow, residual), ('gx', 'gyz'))  17.6 us
    ppermute x18, waiting for transfers between devices, with_halo(): before = lax.ppermute(last, axis, up)  13.9 us
  transfers between devices with their start and end apart: 36, of which 36 were waited for; matrix products, arithmetic and copies ran while one was open for 0% of the time, Pallas kernels for 0%

profile of v1, /device:TPU:0, one launch (start us, length us, event | category | flops | bytes accessed | tf_op | source)
XLA Modules:
  0.0 359.0 jit_solution(3986117640338845528)
XLA Ops:
  1.5 4.9 %collective-permute-start.1 = (f32[2,3,2,8,128]{4,3,2,1,0:T(8,128)S(1)}, f32[2,3,2,8,128]{4,3,2,1,0:T(8,128)S(1)}, u32[]{:S(2)}, u32[]{:S(2)}) collective-permute-start(f32[2,3,2,8,128]{4,3,2,1,0:T(8,128)S(1)} %get-tuple-element.252), channel_id=1, source_target_pairs={{0,4},{1,5},{2,6},{3,7},{8,12},{9,13},{10,14},{11,15},{16,20},{17,... | collective-permute-start | bytes 147464 | tf_op jit(solution)/shard_map/ppermute | solution.py:26
  18.4 4.4 %collective-permute-done.2 = f32[2,3,20,2,128]{4,3,2,1,0:T(2,128)S(1)} collective-permute-done((f32[2,3,20,2,128]{4,3,2,1,0:T(2,128)S(1)}, f32[2,3,20,2,128]{4,3,2,1,0:T(2,128)S(1)}, u32[]{:S(2)}, u32[]{:S(2)}) %collective-permute-start.2) | collective-permute-done | bytes 122912 | tf_op jit(solution)/shard_map/ppermute | solution.py:27
  38.2 4.4 %collective-permute-done.6 = f32[2,3,20,2,128]{4,3,2,1,0:T(2,128)S(1)} collective-permute-done((f32[2,3,20,2,128]{4,3,2,1,0:T(2,128)S(1)}, f32[2,3,20,2,128]{4,3,2,1,0:T(2,128)S(1)}, u32[]{:S(2)}, u32[]{:S(2)}) %collective-permute-start.6) | collective-permute-done | bytes 122912 | tf_op jit(solution)/shard_map/ppermute | solution.py:27
  44.6 9.9 %all-reduce.17 = (f32[3]{0:T(128)S(1)}, f32[3]{0:T(128)S(1)}) all-reduce(f32[3]{0:T(128)S(1)} %get-tuple-element.3, f32[3]{0:T(128)S(1)} %get-tuple-element.2), channel_id=1, replica_groups=mesh['orb'=4,'gx'=2,'gyz'=4] {'gyz'}, use_global_device_ids=true, to_apply=%region_8.9 | all-reduce | flops 6 | bytes 48 | tf_op jit(solution)/shard_map/psum | solution.py:15
  54.5 4.9 %all-reduce.21 = (f32[3]{0:T(128)S(1)}, f32[3]{0:T(128)S(1)}) all-reduce(f32[3]{0:T(128)S(1)} %get-tuple-element.76, f32[3]{0:T(128)S(1)} %get-tuple-element.77), channel_id=1, replica_groups=mesh['orb'=4,'gx'=2,'gyz'=4] {'gx'}, use_global_device_ids=true, to_apply=%region_9.10 | all-reduce | flops 6 | bytes 48 | tf_op jit(solution)/shard_map/psum | solution.py:16
  59.4 17.6 %all-reduce.13 = (f32[3]{0:T(128)S(1)}, f32[3]{0:T(128)S(1)}) all-reduce(f32[3]{0:T(128)S(1)} %get-tuple-element.43, f32[3]{0:T(128)S(1)} %get-tuple-element.42), channel_id=1, replica_groups=mesh['orb'=4,'gx'=2,'gyz'=4] {'gx','gyz'}, use_global_device_ids=true, to_apply=%region_1.2 | all-reduce | flops 6 | bytes 48 | tf_op jit(solution)/shard_map/psum | solution.py:117
  92.1 4.3 %collective-permute-done.10 = f32[2,3,20,2,128]{4,3,2,1,0:T(2,128)S(1)} collective-permute-done((f32[2,3,20,2,128]{4,3,2,1,0:T(2,128)S(1)}, f32[2,3,20,2,128]{4,3,2,1,0:T(2,128)S(1)}, u32[]{:S(2)}, u32[]{:S(2)}) %collective-permute-start.10) | collective-permute-done | bytes 122912 | tf_op jit(solution)/shard_map/ppermute | solution.py:27
  98.8 17.4 %all-reduce.12 = (f32[3]{0:T(128)S(1)}, f32[3]{0:T(128)S(1)}, f32[3]{0:T(128)S(1)}, f32[3]{0:T(128)S(1)}, f32[3]{0:T(128)S(1)}, /*index=5*/f32[3]{0:T(128)S(1)}, f32[3]{0:T(128)S(1)}) all-reduce(f32[3]{0:T(128)S(1)} %get-tuple-element.40, f32[3]{0:T(128)S(1)} %fusion.80, ...), channel_id=1, replica_groups=mesh['orb'=4,'gx'=2,'gyz'=4] {'gx','gyz'}, use_global_device_ids=true, to_apply=%region_15.16 | all-reduce | flops 21 | bytes 168 | tf_op jit(solution)/shard_map/psum | solution.py:129
  132.0 4.4 %collective-permute-done.14 = f32[2,3,20,2,128]{4,3,2,1,0:T(2,128)S(1)} collective-permute-done((f32[2,3,20,2,128]{4,3,2,1,0:T(2,128)S(1)}, f32[2,3,20,2,128]{4,3,2,1,0:T(2,128)S(1)}, u32[]{:S(2)}, u32[]{:S(2)}) %collective-permute-start.14) | collective-permute-done | bytes 122912 | tf_op jit(solution)/shard_map/ppermute | solution.py:27
  138.3 9.1 %all-reduce.16 = (f32[3]{0:T(128)S(1)}, f32[3]{0:T(128)S(1)}) all-reduce(f32[3]{0:T(128)S(1)} %get-tuple-element.23, f32[3]{0:T(128)S(1)} %get-tuple-element.22), channel_id=1, replica_groups=mesh['orb'=4,'gx'=2,'gyz'=4] {'gyz'}, use_global_device_ids=true, to_apply=%region_28.29 | all-reduce | flops 6 | bytes 48 | tf_op jit(solution)/shard_map/psum | solution.py:15
  147.4 4.9 %all-reduce.20 = (f32[3]{0:T(128)S(1)}, f32[3]{0:T(128)S(1)}) all-reduce(f32[3]{0:T(128)S(1)} %get-tuple-element.74, f32[3]{0:T(128)S(1)} %get-tuple-element.75), channel_id=1, replica_groups=mesh['orb'=4,'gx'=2,'gyz'=4] {'gx'}, use_global_device_ids=true, to_apply=%region_29.30 | all-reduce | flops 6 | bytes 48 | tf_op jit(solution)/shard_map/psum | solution.py:16
  157.7 4.3 %collective-permute-done.16 = f32[2,3,2,8,128]{4,3,2,1,0:T(8,128)S(1)} collective-permute-done((f32[2,3,2,8,128]{4,3,2,1,0:T(8,128)S(1)}, f32[2,3,2,8,128]{4,3,2,1,0:T(8,128)S(1)}, u32[]{:S(2)}, u32[]{:S(2)}) %collective-permute-start.16) | collective-permute-done | bytes 49184 | tf_op jit(solution)/shard_map/ppermute | solution.py:27
  167.7 4.4 %collective-permute-done.18 = f32[2,3,20,2,128]{4,3,2,1,0:T(2,128)S(1)} collective-permute-done((f32[2,3,20,2,128]{4,3,2,1,0:T(2,128)S(1)}, f32[2,3,20,2,128]{4,3,2,1,0:T(2,128)S(1)}, u32[]{:S(2)}, u32[]{:S(2)}) %collective-permute-start.18) | collective-permute-done | bytes 122912 | tf_op jit(solution)/shard_map/ppermute | solution.py:27
  175.0 17.4 %all-reduce.11 = (f32[3]{0:T(128)S(1)}, f32[3]{0:T(128)S(1)}, f32[3]{0:T(128)S(1)}, f32[3]{0:T(128)S(1)}, f32[3]{0:T(128)S(1)}, /*index=5*/f32[3]{0:T(128)S(1)}, f32[3]{0:T(128)S(1)}) all-reduce(f32[3]{0:T(128)} %get-tuple-element.36, f32[3]{0:T(128)S(1)} %fusion.81, ...), channel_id=1, replica_groups=mesh['orb'=4,'gx'=2,'gyz'=4] {'gx','gyz'}, use_global_device_ids=true, to_apply=%region_35.36 | all-reduce | flops 21 | bytes 168 | tf_op jit(solution)/shard_map/psum | solution.py:129
  210.9 4.4 %collective-permute-done.22 = f32[2,3,20,2,128]{4,3,2,1,0:T(2,128)S(1)} collective-permute-done((f32[2,3,20,2,128]{4,3,2,1,0:T(2,128)S(1)}, f32[2,3,20,2,128]{4,3,2,1,0:T(2,128)S(1)}, u32[]{:S(2)}, u32[]{:S(2)}) %collective-permute-start.22) | collective-permute-done | bytes 122912 | tf_op jit(solution)/shard_map/ppermute | solution.py:27
  217.2 8.9 %all-reduce.15 = (f32[3]{0:T(128)S(1)}, f32[3]{0:T(128)S(1)}) all-reduce(f32[3]{0:T(128)S(1)} %get-tuple-element.15, f32[3]{0:T(128)S(1)} %get-tuple-element.14), channel_id=1, replica_groups=mesh['orb'=4,'gx'=2,'gyz'=4] {'gyz'}, use_global_device_ids=true, to_apply=%region_48.49 | all-reduce | flops 6 | bytes 48 | tf_op jit(solution)/shard_map/psum | solution.py:15
  226.1 4.9 %all-reduce.19 = (f32[3]{0:T(128)S(1)}, f32[3]{0:T(128)S(1)}) all-reduce(f32[3]{0:T(128)S(1)} %get-tuple-element.72, f32[3]{0:T(128)S(1)} %get-tuple-element.73), channel_id=1, replica_groups=mesh['orb'=4,'gx'=2,'gyz'=4] {'gx'}, use_global_device_ids=true, to_apply=%region_49.50 | all-reduce | flops 6 | bytes 48 | tf_op jit(solution)/shard_map/psum | solution.py:16
  247.5 4.7 %collective-permute-done.26 = f32[2,3,20,2,128]{4,3,2,1,0:T(2,128)S(1)} collective-permute-done((f32[2,3,20,2,128]{4,3,2,1,0:T(2,128)S(1)}, f32[2,3,20,2,128]{4,3,2,1,0:T(2,128)S(1)}, u32[]{:S(2)}, u32[]{:S(2)}) %collective-permute-start.26) | collective-permute-done | bytes 122912 | tf_op jit(solution)/shard_map/ppermute | solution.py:27
  255.7 17.9 %all-reduce.10 = (f32[3]{0:T(128)}, f32[3]{0:T(128)}, f32[3]{0:T(128)}, f32[3]{0:T(128)}, f32[3]{0:T(128)}, /*index=5*/f32[3]{0:T(128)}, f32[3]{0:T(128)}) all-reduce(f32[3]{0:T(128)} %get-tuple-element.32, f32[3]{0:T(128)} %fusion.82, f32[3]{0:T(128)} %get-tuple-element.33, ...), channel_id=1, replica_groups=mesh['orb'=4,'gx'=2,'gyz'=4] {'gx','gyz'}, use_global_device_ids=true, to_apply=%region_55.56 | all-reduce | flops 21 | bytes 168 | tf_op jit(solution)/shard_map/psum | solution.py:129
  291.8 4.4 %collective-permute-done.30 = f32[2,3,20,2,128]{4,3,2,1,0:T(2,128)S(1)} collective-permute-done((f32[2,3,20,2,128]{4,3,2,1,0:T(2,128)S(1)}, f32[2,3,20,2,128]{4,3,2,1,0:T(2,128)S(1)}, u32[]{:S(2)}, u32[]{:S(2)}) %collective-permute-start.30) | collective-permute-done | bytes 122912 | tf_op jit(solution)/shard_map/ppermute | solution.py:27
  298.6 9.1 %all-reduce.14 = (f32[3]{0:T(128)S(1)}, f32[3]{0:T(128)S(1)}) all-reduce(f32[3]{0:T(128)S(1)} %get-tuple-element.7, f32[3]{0:T(128)S(1)} %get-tuple-element.6), channel_id=1, replica_groups=mesh['orb'=4,'gx'=2,'gyz'=4] {'gyz'}, use_global_device_ids=true, to_apply=%region_68.69 | all-reduce | flops 6 | bytes 48 | tf_op jit(solution)/shard_map/psum | solution.py:15
  307.7 4.9 %all-reduce.18 = (f32[3]{0:T(128)S(1)}, f32[3]{0:T(128)S(1)}) all-reduce(f32[3]{0:T(128)S(1)} %get-tuple-element.70, f32[3]{0:T(128)S(1)} %get-tuple-element.71), channel_id=1, replica_groups=mesh['orb'=4,'gx'=2,'gyz'=4] {'gx'}, use_global_device_ids=true, to_apply=%region_69.70 | all-reduce | flops 6 | bytes 48 | tf_op jit(solution)/shard_map/psum | solution.py:16
  330.1 4.4 %collective-permute-done.34 = f32[2,3,20,2,128]{4,3,2,1,0:T(2,128)S(1)} collective-permute-done((f32[2,3,20,2,128]{4,3,2,1,0:T(2,128)S(1)}, f32[2,3,20,2,128]{4,3,2,1,0:T(2,128)S(1)}, u32[]{:S(2)}, u32[]{:S(2)}) %collective-permute-start.34) | collective-permute-done | bytes 122912 | tf_op jit(solution)/shard_map/ppermute | solution.py:27
  337.3 17.2 %all-reduce.9 = (f32[3]{0:T(128)S(1)}, f32[3]{0:T(128)S(1)}, f32[3]{0:T(128)S(1)}) all-reduce(f32[3]{0:T(128)S(1)} %get-tuple-element.5, f32[3]{0:T(128)S(1)} %fusion.83, f32[3]{0:T(128)S(1)} %get-tuple-element.4), channel_id=1, replica_groups=mesh['orb'=4,'gx'=2,'gyz'=4] {'gx','gyz'}, use_global_device_ids=true, to_apply=%region_75.76 | all-reduce | flops 9 | bytes 72 | tf_op jit(solution)/shard_map/psum | solution.py:129
  (252 shorter events, 164.4 us)
Async XLA Ops:
  1.5 6.6 %collective-permute-start.1 = (f32[2,3,2,8,128]{4,3,2,1,0:T(8,128)S(1)}, f32[2,3,2,8,128]{4,3,2,1,0:T(8,128)S(1)}, u32[]{:S(2)}, u32[]{:S(2)}) collective-permute-start(f32[2,3,2,8,128]{4,3,2,1,0:T(8,128)S(1)} %get-tuple-element.252), channel_id=1, source_target_pairs={{0,4},{1,5},{2,6},{3,7},{8,12},{9,13},{10,14},{11,15},{16,20},{17,... | collective-permute-start | bytes 147464 | tf_op jit(solution)/shard_map/ppermute | solution.py:26
  6.4 6.0 %collective-permute-start = (f32[2,3,2,8,128]{4,3,2,1,0:T(8,128)S(1)}, f32[2,3,2,8,128]{4,3,2,1,0:T(8,128)S(1)}, u32[]{:S(2)}, u32[]{:S(2)}) collective-permute-start(f32[2,3,2,8,128]{4,3,2,1,0:T(8,128)S(1)} %get-tuple-element.251), channel_id=1, source_target_pairs={{4,0},{5,1},{6,2},{7,3},{12,8},{13,9},{14,10},{15,11},{20,16},{21,... | collective-permute-start | bytes 147464 | tf_op jit(solution)/shard_map/ppermute | solution.py:27
  12.5 5.9 %collective-permute-start.3 = (f32[2,3,20,2,128]{4,3,2,1,0:T(2,128)S(1)}, f32[2,3,20,2,128]{4,3,2,1,0:T(2,128)S(1)}, u32[]{:S(2)}, u32[]{:S(2)}) collective-permute-start(f32[2,3,20,2,128]{4,3,2,1,0:T(2,128)S(1)} %get-tuple-element.166), channel_id=1, source_target_pairs={{0,1},{1,2},{2,3},{4,5},{5,6},{6,7},{8,9},{9,10},{10,11},{12,13},{... | collective-permute-start | bytes 368648 | tf_op jit(solution)/shard_map/ppermute | solution.py:26
  16.0 6.8 %collective-permute-start.2 = (f32[2,3,20,2,128]{4,3,2,1,0:T(2,128)S(1)}, f32[2,3,20,2,128]{4,3,2,1,0:T(2,128)S(1)}, u32[]{:S(2)}, u32[]{:S(2)}) collective-permute-start(f32[2,3,20,2,128]{4,3,2,1,0:T(2,128)S(1)} %get-tuple-element.167), channel_id=1, source_target_pairs={{1,0},{2,1},{3,2},{5,4},{6,5},{7,6},{9,8},{10,9},{11,10},{13,12},{... | collective-permute-start | bytes 368648 | tf_op jit(solution)/shard_map/ppermute | solution.py:27
  26.2 6.0 %collective-permute-start.4 = (f32[2,3,2,8,128]{4,3,2,1,0:T(8,128)S(1)}, f32[2,3,2,8,128]{4,3,2,1,0:T(8,128)S(1)}, u32[]{:S(2)}, u32[]{:S(2)}) collective-permute-start(f32[2,3,2,8,128]{4,3,2,1,0:T(8,128)S(1)} %get-tuple-element.247), channel_id=1, source_target_pairs={{4,0},{5,1},{6,2},{7,3},{12,8},{13,9},{14,10},{15,11},{20,16},{21,... | collective-permute-start | bytes 147464 | tf_op jit(solution)/shard_map/ppermute | solution.py:27
  32.2 5.9 %collective-permute-start.7 = (f32[2,3,20,2,128]{4,3,2,1,0:T(2,128)S(1)}, f32[2,3,20,2,128]{4,3,2,1,0:T(2,128)S(1)}, u32[]{:S(2)}, u32[]{:S(2)}) collective-permute-start(f32[2,3,20,2,128]{4,3,2,1,0:T(2,128)S(1)} %get-tuple-element.164), channel_id=1, source_target_pairs={{0,1},{1,2},{2,3},{4,5},{5,6},{6,7},{8,9},{9,10},{10,11},{12,13},{... | collective-permute-start | bytes 368648 | tf_op jit(solution)/shard_map/ppermute | solution.py:26
  35.7 6.8 %collective-permute-start.6 = (f32[2,3,20,2,128]{4,3,2,1,0:T(2,128)S(1)}, f32[2,3,20,2,128]{4,3,2,1,0:T(2,128)S(1)}, u32[]{:S(2)}, u32[]{:S(2)}) collective-permute-start(f32[2,3,20,2,128]{4,3,2,1,0:T(2,128)S(1)} %get-tuple-element.165), channel_id=1, source_target_pairs={{1,0},{2,1},{3,2},{5,4},{6,5},{7,6},{9,8},{10,9},{11,10},{13,12},{... | collective-permute-start | bytes 368648 | tf_op jit(solution)/shard_map/ppermute | solution.py:27
  81.5 6.0 %collective-permute-start.8 = (f32[2,3,2,8,128]{4,3,2,1,0:T(8,128)S(1)}, f32[2,3,2,8,128]{4,3,2,1,0:T(8,128)S(1)}, u32[]{:S(2)}, u32[]{:S(2)}) collective-permute-start(f32[2,3,2,8,128]{4,3,2,1,0:T(8,128)S(1)} %get-tuple-element.241), channel_id=1, source_target_pairs={{4,0},{5,1},{6,2},{7,3},{12,8},{13,9},{14,10},{15,11},{20,16},{21,... | collective-permute-start | bytes 147464 | tf_op jit(solution)/shard_map/ppermute | solution.py:27
  89.6 6.8 %collective-permute-start.10 = (f32[2,3,20,2,128]{4,3,2,1,0:T(2,128)S(1)}, f32[2,3,20,2,128]{4,3,2,1,0:T(2,128)S(1)}, u32[]{:S(2)}, u32[]{:S(2)}) collective-permute-start(f32[2,3,20,2,128]{4,3,2,1,0:T(2,128)S(1)} %get-tuple-element.163), channel_id=1, source_target_pairs={{1,0},{2,1},{3,2},{5,4},{6,5},{7,6},{9,8},{10,9},{11,10},{13,12},{... | collective-permute-start | bytes 368648 | tf_op jit(solution)/shard_map/ppermute | solution.py:27
  121.6 6.0 %collective-permute-start.12 = (f32[2,3,2,8,128]{4,3,2,1,0:T(8,128)S(1)}, f32[2,3,2,8,128]{4,3,2,1,0:T(8,128)S(1)}, u32[]{:S(2)}, u32[]{:S(2)}) collective-permute-start(f32[2,3,2,8,128]{4,3,2,1,0:T(8,128)S(1)} %get-tuple-element.235), channel_id=1, source_target_pairs={{4,0},{5,1},{6,2},{7,3},{12,8},{13,9},{14,10},{15,11},{20,16},{21,... | collective-permute-start | bytes 147464 | tf_op jit(solution)/shard_map/ppermute | solution.py:27
  129.5 6.8 %collective-permute-start.14 = (f32[2,3,20,2,128]{4,3,2,1,0:T(2,128)S(1)}, f32[2,3,20,2,128]{4,3,2,1,0:T(2,128)S(1)}, u32[]{:S(2)}, u32[]{:S(2)}) collective-permute-start(f32[2,3,20,2,128]{4,3,2,1,0:T(2,128)S(1)} %get-tuple-element.161), channel_id=1, source_target_pairs={{1,0},{2,1},{3,2},{5,4},{6,5},{7,6},{9,8},{10,9},{11,10},{13,12},{... | collective-permute-start | bytes 368648 | tf_op jit(solution)/shard_map/ppermute | solution.py:27
  156.0 6.0 %collective-permute-start.16 = (f32[2,3,2,8,128]{4,3,2,1,0:T(8,128)S(1)}, f32[2,3,2,8,128]{4,3,2,1,0:T(8,128)S(1)}, u32[]{:S(2)}, u32[]{:S(2)}) collective-permute-start(f32[2,3,2,8,128]{4,3,2,1,0:T(8,128)S(1)} %get-tuple-element.231), channel_id=1, source_target_pairs={{4,0},{5,1},{6,2},{7,3},{12,8},{13,9},{14,10},{15,11},{20,16},{21,... | collective-permute-start | bytes 147464 | tf_op jit(solution)/shard_map/ppermute | solution.py:27
  162.1 5.6 %collective-permute-start.19 = (f32[2,3,20,2,128]{4,3,2,1,0:T(2,128)S(1)}, f32[2,3,20,2,128]{4,3,2,1,0:T(2,128)S(1)}, u32[]{:S(2)}, u32[]{:S(2)}) collective-permute-start(f32[2,3,20,2,128]{4,3,2,1,0:T(2,128)S(1)} %get-tuple-element.158), channel_id=1, source_target_pairs={{0,1},{1,2},{2,3},{4,5},{5,6},{6,7},{8,9},{9,10},{10,11},{12,13},{... | collective-permute-start | bytes 368648 | tf_op jit(solution)/shard_map/ppermute | solution.py:26
  165.2 6.8 %collective-permute-start.18 = (f32[2,3,20,2,128]{4,3,2,1,0:T(2,128)S(1)}, f32[2,3,20,2,128]{4,3,2,1,0:T(2,128)S(1)}, u32[]{:S(2)}, u32[]{:S(2)}) collective-permute-start(f32[2,3,20,2,128]{4,3,2,1,0:T(2,128)S(1)} %get-tuple-element.159), channel_id=1, source_target_pairs={{1,0},{2,1},{3,2},{5,4},{6,5},{7,6},{9,8},{10,9},{11,10},{13,12},{... | collective-permute-start | bytes 368648 | tf_op jit(solution)/shard_map/ppermute | solution.py:27
  199.9 6.0 %collective-permute-start.20 = (f32[2,3,2,8,128]{4,3,2,1,0:T(8,128)S(1)}, f32[2,3,2,8,128]{4,3,2,1,0:T(8,128)S(1)}, u32[]{:S(2)}, u32[]{:S(2)}) collective-permute-start(f32[2,3,2,8,128]{4,3,2,1,0:T(8,128)S(1)} %get-tuple-element.225), channel_id=1, source_target_pairs={{4,0},{5,1},{6,2},{7,3},{12,8},{13,9},{14,10},{15,11},{20,16},{21,... | collective-permute-start | bytes 147464 | tf_op jit(solution)/shard_map/ppermute | solution.py:27
  208.5 6.8 %collective-permute-start.22 = (f32[2,3,20,2,128]{4,3,2,1,0:T(2,128)S(1)}, f32[2,3,20,2,128]{4,3,2,1,0:T(2,128)S(1)}, u32[]{:S(2)}, u32[]{:S(2)}) collective-permute-start(f32[2,3,20,2,128]{4,3,2,1,0:T(2,128)S(1)} %get-tuple-element.157), channel_id=1, source_target_pairs={{1,0},{2,1},{3,2},{5,4},{6,5},{7,6},{9,8},{10,9},{11,10},{13,12},{... | collective-permute-start | bytes 368648 | tf_op jit(solution)/shard_map/ppermute | solution.py:27
  234.8 6.0 %collective-permute-start.24 = (f32[2,3,2,8,128]{4,3,2,1,0:T(8,128)S(1)}, f32[2,3,2,8,128]{4,3,2,1,0:T(8,128)S(1)}, u32[]{:S(2)}, u32[]{:S(2)}) collective-permute-start(f32[2,3,2,8,128]{4,3,2,1,0:T(8,128)S(1)} %get-tuple-element.221), channel_id=1, source_target_pairs={{4,0},{5,1},{6,2},{7,3},{12,8},{13,9},{14,10},{15,11},{20,16},{21,... | collective-permute-start | bytes 147464 | tf_op jit(solution)/shard_map/ppermute | solution.py:27
  240.9 6.6 %collective-permute-start.27 = (f32[2,3,20,2,128]{4,3,2,1,0:T(2,128)S(1)}, f32[2,3,20,2,128]{4,3,2,1,0:T(2,128)S(1)}, u32[]{:S(2)}, u32[]{:S(2)}) collective-permute-start(f32[2,3,20,2,128]{4,3,2,1,0:T(2,128)S(1)} %get-tuple-element.154), channel_id=1, source_target_pairs={{0,1},{1,2},{2,3},{4,5},{5,6},{6,7},{8,9},{9,10},{10,11},{12,13},{... | collective-permute-start | bytes 368648 | tf_op jit(solution)/shard_map/ppermute | solution.py:26
  244.2 7.9 %collective-permute-start.26 = (f32[2,3,20,2,128]{4,3,2,1,0:T(2,128)S(1)}, f32[2,3,20,2,128]{4,3,2,1,0:T(2,128)S(1)}, u32[]{:S(2)}, u32[]{:S(2)}) collective-permute-start(f32[2,3,20,2,128]{4,3,2,1,0:T(2,128)S(1)} %get-tuple-element.155), channel_id=1, source_target_pairs={{1,0},{2,1},{3,2},{5,4},{6,5},{7,6},{9,8},{10,9},{11,10},{13,12},{... | collective-permute-start | bytes 368648 | tf_op jit(solution)/shard_map/ppermute | solution.py:27
  280.5 6.0 %collective-permute-start.28 = (f32[2,3,2,8,128]{4,3,2,1,0:T(8,128)S(1)}, f32[2,3,2,8,128]{4,3,2,1,0:T(8,128)S(1)}, u32[]{:S(2)}, u32[]{:S(2)}) collective-permute-start(f32[2,3,2,8,128]{4,3,2,1,0:T(8,128)S(1)} %get-tuple-element.215), channel_id=1, source_target_pairs={{4,0},{5,1},{6,2},{7,3},{12,8},{13,9},{14,10},{15,11},{20,16},{21,... | collective-permute-start | bytes 147464 | tf_op jit(solution)/shard_map/ppermute | solution.py:27
  289.3 6.8 %collective-permute-start.30 = (f32[2,3,20,2,128]{4,3,2,1,0:T(2,128)S(1)}, f32[2,3,20,2,128]{4,3,2,1,0:T(2,128)S(1)}, u32[]{:S(2)}, u32[]{:S(2)}) collective-permute-start(f32[2,3,20,2,128]{4,3,2,1,0:T(2,128)S(1)} %get-tuple-element.153), channel_id=1, source_target_pairs={{1,0},{2,1},{3,2},{5,4},{6,5},{7,6},{9,8},{10,9},{11,10},{13,12},{... | collective-permute-start | bytes 368648 | tf_op jit(solution)/shard_map/ppermute | solution.py:27
  318.4 6.0 %collective-permute-start.32 = (f32[2,3,2,8,128]{4,3,2,1,0:T(8,128)S(1)}, f32[2,3,2,8,128]{4,3,2,1,0:T(8,128)S(1)}, u32[]{:S(2)}, u32[]{:S(2)}) collective-permute-start(f32[2,3,2,8,128]{4,3,2,1,0:T(8,128)S(1)} %get-tuple-element.211), channel_id=1, source_target_pairs={{4,0},{5,1},{6,2},{7,3},{12,8},{13,9},{14,10},{15,11},{20,16},{21,... | collective-permute-start | bytes 147464 | tf_op jit(solution)/shard_map/ppermute | solution.py:27
  324.5 5.6 %collective-permute-start.35 = (f32[2,3,20,2,128]{4,3,2,1,0:T(2,128)S(1)}, f32[2,3,20,2,128]{4,3,2,1,0:T(2,128)S(1)}, u32[]{:S(2)}, u32[]{:S(2)}) collective-permute-start(f32[2,3,20,2,128]{4,3,2,1,0:T(2,128)S(1)} %get-tuple-element.150), channel_id=1, source_target_pairs={{0,1},{1,2},{2,3},{4,5},{5,6},{6,7},{8,9},{9,10},{10,11},{12,13},{... | collective-permute-start | bytes 368648 | tf_op jit(solution)/shard_map/ppermute | solution.py:26
  327.6 6.8 %collective-permute-start.34 = (f32[2,3,20,2,128]{4,3,2,1,0:T(2,128)S(1)}, f32[2,3,20,2,128]{4,3,2,1,0:T(2,128)S(1)}, u32[]{:S(2)}, u32[]{:S(2)}) collective-permute-start(f32[2,3,20,2,128]{4,3,2,1,0:T(2,128)S(1)} %get-tuple-element.151), channel_id=1, source_target_pairs={{1,0},{2,1},{3,2},{5,4},{6,5},{7,6},{9,8},{10,9},{11,10},{13,12},{... | collective-permute-start | bytes 368648 | tf_op jit(solution)/shard_map/ppermute | solution.py:27
  (50 other events, 276.0 us)
